TPU v7x, 32 devices: a 4x4x1 block of a 4x4x8 slice. The times are simulated.
32 devices in a mesh: dp: 2 (over z, core), ep: 16 (over x, y).
Axes of the slice: x: 4, y: 4, z: 1, core: 2. Of those that a mesh axis runs over, the one named last changes fastest.
The devices are a block of a 4x4x8 slice.
Arguments:
- x: bfloat16 [2, 16, 256, 2560], P('dp', 'ep'), parts along dimension 0
- expert: int32 [2, 16, 256, 6], P('dp', 'ep'), parts along dimension 0
- slot: int32 [2, 16, 256, 6], P('dp', 'ep'), parts along dimension 0
- gate: float32 [2, 16, 256, 6], P('dp', 'ep'), parts along dimension 0
- w_gate: bfloat16 [80, 2560, 1536], P('ep')
- w_up: bfloat16 [80, 2560, 1536], P('ep')
- w_down: bfloat16 [80, 1536, 2560], P('ep')
- s_gate: bfloat16 [2560, 3072], replicated
- s_up: bfloat16 [2560, 3072], replicated
- s_down: bfloat16 [3072, 2560], replicated
Outputs:
- y: bfloat16 [2, 16, 256, 2560], P('dp', 'ep'), parts along dimension 0
There are 2 independent parts. A program takes and returns all parts, laid end to end along the dimension named above; an argument that names none is the same for every part.
All inputs are finite; a program needn't handle non-finite values.
Results may differ from a plain program's by a relative error of at most 0.009.
Values are sent between devices in bfloat16 or wider.
A program may use at most 768 MiB of HBM per device.

v0:
```python
import jax
import jax.numpy as jnp
from jax import lax
from jax.sharding import NamedSharding, PartitionSpec as P


def einsum(form, a, b):
    return jnp.einsum(form, a.astype(jnp.float32), b.astype(jnp.float32))


def for_all(x, s_gate, s_up, s_down):
    h = jax.nn.silu(einsum("...d,df->...f", x, s_gate)) * einsum("...d,df->...f", x, s_up)
    return einsum("...f,fd->...d", h.astype(jnp.bfloat16), s_down)


def solution(mesh):
    def placed(v, *spec):
        return lax.with_sharding_constraint(v, NamedSharding(mesh, P(*spec)))

    def step(x, expert, slot, gate, w_gate, w_up, w_down, s_gate, s_up, s_down):
        experts, (tokens, top) = w_gate.shape[0], expert.shape[2:]
        slots = 5 * tokens * top // (4 * experts)
        to_expert = jax.nn.one_hot(expert, experts, dtype=jnp.bfloat16)
        to_slot = jax.nn.one_hot(slot, slots, dtype=jnp.bfloat16)
        weighted = to_expert * gate[..., None].astype(jnp.bfloat16)
        dispatch = einsum("abtke,abtkc->abtec", to_expert, to_slot).astype(jnp.bfloat16)
        combine = einsum("abtke,abtkc->abtec", weighted, to_slot).astype(jnp.bfloat16)
        z = einsum("abtec,abtd->aebcd", dispatch, x).astype(jnp.bfloat16)
        z = placed(z, "dp", None, "ep", None, None)
        z = placed(z, "dp", "ep", None, None, None)
        h = jax.nn.silu(einsum("aebcd,edf->aebcf", z, w_gate))
        h = (h * einsum("aebcd,edf->aebcf", z, w_up)).astype(jnp.bfloat16)
        out = einsum("aebcf,efd->aebcd", h, w_down).astype(jnp.bfloat16)
        out = placed(out, "dp", "ep", None, None, None)
        out = placed(out, "dp", None, "ep", None, None)
        y = einsum("abtec,aebcd->abtd", combine, out)
        return (y + for_all(x, s_gate, s_up, s_down)).astype(jnp.bfloat16)

    return step
```

profile of v0, /device:TPU:96, one launch (start us, length us, event | category | flops | bytes accessed | tf_op | source)
XLA Modules:
  0.0 400.8 jit_solution(5027993171286104578)
XLA Ops:
  0.0 0.0 copy-start
  0.0 0.9 copy.25
  0.9 0.0 copy-start.1
  0.9 0.8 copy.27
  1.8 0.0 copy-start.3
  1.8 0.0 copy-done.1
  1.8 0.6 copy-done.3
  2.5 3.6 convolution_convert_fusion.1
  6.1 2.4 copy.13
  8.6 0.0 copy-done
  8.6 3.0 convolution_convert_fusion
  11.6 128.5 %all-to-all.4 = bf16[1,16,5,1,24,2560]{5,4,2,3,0,1:T(8,128)(2,1)} all-to-all(bf16[1,16,5,1,24,2560]{5,4,2,3,0,1:T(8,128)(2,1)S(1)} %bitcast.105), channel_id=1, replica_groups=mesh['dp'=2,'ep'=16] {'ep'}, dimensions={1} | all-to-all | bytes 19660800 | tf_op jit(solution)/sharding_constraint;jit(solution)/sharding_constraint | solution.py:18
  140.0 29.9 %fusion.2 = f32[5,16,24,1536]{3,2,1,0:T(8,128)} fusion(bf16[5,2560,1536]{2,1,0:T(8,128)(2,1)} %param.5, bf16[1,16,5,1,24,2560]{5,4,2,3,0,1:T(8,128)(2,1)} %all-to-all.4), kind=kOutput, calls=%fused_computation.2 | convolution fusion | flops 15099494400 | bytes 60948480 | tf_op jit(solution)/aebcd,edf->aebcf/dot_general | solution.py:8
  169.9 30.1 %fusion.4 = f32[5,16,24,1536]{3,2,1,0:T(8,128)} fusion(bf16[5,2560,1536]{2,1,0:T(8,128)(2,1)} %param.4, bf16[1,16,5,1,24,2560]{5,4,2,3,0,1:T(8,128)(2,1)} %all-to-all.4), kind=kOutput, calls=%fused_computation.4 | convolution fusion | flops 15099494400 | bytes 60948480 | tf_op jit(solution)/aebcd,edf->aebcf/dot_general | solution.py:8
  200.0 28.3 %convert_bitcast_fusion = bf16[1,5,16,1,24,2560]{5,4,2,1,3,0:T(8,128)(2,1)} fusion(bf16[5,1536,2560]{2,1,0:T(8,128)(2,1)} %param.6, f32[5,16,24,1536]{3,2,1,0:T(8,128)} %fusion.2, f32[5,16,24,1536]{3,2,1,0:T(8,128)} %fusion.4), kind=kOutput, calls=%fused_computation.15 | convolution fusion | flops 15122104320 | bytes 72744960 | tf_op jit(solution)/aebcf,efd->aebcd/dot_general | solution.py:8
  228.3 8.2 %copy.16 = bf16[1,5,16,1,24,2560]{5,4,1,3,0,2:T(8,128)(2,1)} copy(bf16[1,5,16,1,24,2560]{5,4,2,1,3,0:T(8,128)(2,1)} %convert_bitcast_fusion) | data formatting | bytes 19660800 | tf_op jit(solution)/sharding_constraint;jit(solution)/sharding_constraint | solution.py:18
  236.6 0.0 copy-start.5
  236.6 0.0 copy-start.2
  236.6 0.0 copy-start.4
  236.6 5.5 %all-to-all-start.1 = ((bf16[1,5,16,1,24,2560]{5,4,1,3,0,2:T(8,128)(2,1)}), bf16[1,5,16,1,24,2560]{5,4,1,3,0,2:T(8,128)(2,1)}, u32[]{:S(2)}, u32[]{:S(2)}) async-start(bf16[1,5,16,1,24,2560]{5,4,1,3,0,2:T(8,128)(2,1)} %copy.16), calls=%async_computation.1 | async-start | bytes 19660800 | tf_op jit(solution)/sharding_constraint;jit(solution)/sharding_constraint | solution.py:18
  242.1 0.0 copy-done.5
  242.2 0.1 copy.26
  242.3 0.0 copy-done.2
  242.3 0.0 copy-done.4
  242.3 3.9 convolution_convert_fusion.2
  246.2 2.4 copy.23
  248.7 7.7 %convolution_bitcast_fusion.1 = f32[1,1,256,3072]{3,2,1,0:T(8,128)S(1)} fusion(bf16[2560,3072]{1,0:T(8,128)(2,1)} %param.7, bf16[1,1,256,2560]{3,2,1,0:T(8,128)(2,1)S(1)} %copy-done), kind=kOutput, calls=%fused_computation.21 | convolution fusion | flops 4026531840 | bytes 20185088 | tf_op jit(solution)/...d,df->...f/dot_general | solution.py:8
  256.4 11.3 %fusion.21 = bf16[256,3072]{1,0:T(8,128)(2,1)} fusion(bf16[2560,3072]{1,0:T(8,128)(2,1)} %param.8, f32[1,1,256,3072]{3,2,1,0:T(8,128)S(1)} %convolution_bitcast_fusion.1, bf16[1,1,256,2560]{3,2,1,0:T(8,128)(2,1)S(1)} %copy-done), kind=kOutput, calls=%fused_computation.27 | convolution fusion | flops 4031250432 | bytes 21757952 | tf_op jit(solution)/...d,df->...f/dot_general | solution.py:8
  267.6 118.3 %all-to-all-done.1 = bf16[1,5,16,1,24,2560]{5,4,1,3,0,2:T(8,128)(2,1)} async-done(((bf16[1,5,16,1,24,2560]{5,4,1,3,0,2:T(8,128)(2,1)}), bf16[1,5,16,1,24,2560]{5,4,1,3,0,2:T(8,128)(2,1)}, u32[]{:S(2)}, u32[]{:S(2)}) %all-to-all-start.1) | async-done | bytes 9830432 | tf_op jit(solution)/sharding_constraint;jit(solution)/sharding_constraint | solution.py:18
  385.9 0.0 copy-start.6
  385.9 5.6 %convolution_bitcast_fusion.2 = f32[256,2560]{1,0:T(8,128)S(1)} fusion(bf16[256,80,24]{0,2,1:T(8,128)(2,1)S(1)} %copy.23, bf16[80,24,2560]{2,1,0:T(8,128)(2,1)} %bitcast.25), kind=kOutput, calls=%fused_computation.23 | convolution fusion | flops 2516582400 | bytes 13434880 | tf_op jit(solution)/abtec,aebcd->abtd/dot_general | solution.py:8
  391.6 0.0 copy-done.6
  391.6 9.1 %fusion.22 = bf16[1,1,256,2560]{3,2,1,0:T(8,128)(2,1)} fusion(f32[256,2560]{1,0:T(8,128)S(1)} %convolution_bitcast_fusion.2, bf16[256,3072]{1,0:T(8,128)(2,1)S(1)} %copy-done.6, bf16[3072,2560]{1,0:T(8,128)(2,1)} %param.9), kind=kOutput, calls=%fused_computation.28 | convolution fusion | flops 4027842560 | bytes 21233664 | tf_op jit(solution)/...f,fd->...d/dot_general | solution.py:8
  (1 shorter events, 0.0 us)
Async XLA Ops:
  0.0 8.6 %copy-start = (bf16[1,1,256,2560]{3,2,1,0:T(8,128)(2,1)S(1)}, bf16[1,1,256,2560]{3,2,1,0:T(8,128)(2,1)}, u32[]{:S(2)}) copy-start(bf16[1,1,256,2560]{3,2,1,0:T(8,128)(2,1)} %param.3) | copy-start | bytes 3932164
  0.9 0.9 copy-start.1
  1.8 0.7 copy-start.3
  236.6 5.6 %copy-start.5 = (f32[1,1,256,6]{2,1,3,0:T(1,128)S(1)}, f32[1,1,256,6]{2,1,3,0:T(1,128)}, u32[]{:S(2)}) copy-start(f32[1,1,256,6]{2,1,3,0:T(1,128)} %param.1) | copy-start | bytes 18436
  236.6 5.7 %copy-start.2 = (s32[1,1,256,6]{3,2,1,0:T(8,128)S(1)}, s32[1,1,256,6]{3,2,1,0:T(8,128)}, u32[]{:S(2)}) copy-start(s32[1,1,256,6]{3,2,1,0:T(8,128)} %copy-done.1) | copy-start | bytes 18436
  236.6 5.7 %copy-start.4 = (s32[1,1,256,6]{3,2,1,0:T(8,128)S(1)}, s32[1,1,256,6]{3,2,1,0:T(8,128)}, u32[]{:S(2)}) copy-start(s32[1,1,256,6]{3,2,1,0:T(8,128)} %copy-done.3) | copy-start | bytes 18436
  236.6 149.4 %all-to-all-start.1 = ((bf16[1,5,16,1,24,2560]{5,4,1,3,0,2:T(8,128)(2,1)}), bf16[1,5,16,1,24,2560]{5,4,1,3,0,2:T(8,128)(2,1)}, u32[]{:S(2)}, u32[]{:S(2)}) async-start(bf16[1,5,16,1,24,2560]{5,4,1,3,0,2:T(8,128)(2,1)} %copy.16), calls=%async_computation.1 | async-start | bytes 19660800 | tf_op jit(solution)/sharding_constraint;jit(solution)/sharding_constraint | solution.py:18
  385.9 5.7 %copy-start.6 = (bf16[256,3072]{1,0:T(8,128)(2,1)S(1)}, bf16[256,3072]{1,0:T(8,128)(2,1)}, u32[]{:S(2)}) copy-start(bf16[256,3072]{1,0:T(8,128)(2,1)} %fusion.21) | copy-start | bytes 4718596
where the time goes:
time: 405 us; the launch traced here: 401 us
  matrix products  133 us (33%)
  blocking collectives  128 us (32%)
  waiting for transfers between devices  118 us (29%)
  local copies, waits for them, and re-layouts  15.7 us (4%)
  starting transfers between devices  5.54 us (1%)
    dot_general x10, matrix products, einsum(): return jnp.einsum(form, a.astype(jnp.float32), b.astype(jnp.float32))  133 us
    another operation x1, blocking collectives, placed(): return lax.with_sharding_constraint(v, NamedSharding(mesh, P(*spec)))  128 us
    another operation x1, waiting for transfers between devices, placed(): return lax.with_sharding_constraint(v, NamedSharding(mesh, P(*spec)))  118 us
    another operation x1, local copies, waits for them, and re-layouts, placed(): return lax.with_sharding_constraint(v, NamedSharding(mesh, P(*spec)))  8.24 us
  transfers between devices with their start and end apart: 1, of which 1 were waited for; matrix products, arithmetic and copies ran while one was open for 6% of the time, Pallas kernels for 0%

commit v1 on v0

v1 whole, which is shorter than its diff:
```python
import functools
import math

import jax
import jax.numpy as jnp
from jax import lax
from jax.experimental import pallas as pl
from jax.experimental.pallas import tpu as pltpu
from jax.sharding import PartitionSpec as P

F32, BF16 = jnp.float32, jnp.bfloat16
LO, HI = 16, 8
CT = 256
DB = 4


def dot(a, b):
    return jnp.dot(a, b, preferred_element_type=F32)


def cols(i):
    return pl.ds(pl.multiple_of(i * CT, CT), CT)


def kernel(
    S, EPD, TOP,
    x_ref, meta_ref, wg, wu, wd, sg, su, sd, y_ref,
    ag, mall, oh, dsend, z, zf, crecv, via, fin, cmat, h, ysh, gu, db,
    gu_sem, db_sem, ag_s, ag_r, m_s, m_r, z_s, z_r, c_s, c_r, v_s, v_r, f_s, f_r,
):
    T, D = x_ref.shape
    FF = wg.shape[2]
    H = D // 2
    SL = LO + HI
    CH = S * SL
    HT = T // 2
    QS = sg.shape[1] // FF
    NG, NDT = FF // CT, D // CT
    HTILES = H // CT
    me = lax.axis_index("ep")
    px, py = lax.div(me, S), lax.rem(me, S)

    def dev(p, df, ds):
        dx = df * (1 - p) + ds * p
        dy = df * p + ds * (1 - p)
        return lax.rem(px + dx, S) * S + lax.rem(py + dy, S)

    def start_gu(n):
        slot = lax.rem(n, 2)

        @pl.when(n < QS * NG)
        def _():
            c = cols(n)
            pltpu.make_async_copy(sg.at[:, c], gu.at[slot, 0], gu_sem.at[slot, 0]).start()
            pltpu.make_async_copy(su.at[:, c], gu.at[slot, 1], gu_sem.at[slot, 1]).start()

        @pl.when(jnp.logical_and(n >= QS * NG, n < (QS + EPD) * NG))
        def _():
            k = n - QS * NG
            e, c = lax.div(k, NG), cols(lax.rem(k, NG))
            pltpu.make_async_copy(wg.at[e, :, c], gu.at[slot, 0], gu_sem.at[slot, 0]).start()
            pltpu.make_async_copy(wu.at[e, :, c], gu.at[slot, 1], gu_sem.at[slot, 1]).start()

    def wait_gu(n):
        slot = lax.rem(n, 2)
        for j in range(2):
            pltpu.make_async_copy(sg.at[:, cols(0)], gu.at[slot, j], gu_sem.at[slot, j]).wait()
        return slot

    def start_db(m):
        slot = lax.rem(m, DB)

        @pl.when(m < QS * NDT)
        def _():
            q, c = lax.div(m, NDT), cols(lax.rem(m, NDT))
            rows = pl.ds(pl.multiple_of(q * FF, FF), FF)
            pltpu.make_async_copy(sd.at[rows, c], db.at[slot], db_sem.at[slot]).start()

        @pl.when(jnp.logical_and(m >= QS * NDT, m < (QS + EPD) * NDT))
        def _():
            k = m - QS * NDT
            pltpu.make_async_copy(
                wd.at[lax.div(k, NDT), :, cols(lax.rem(k, NDT))], db.at[slot], db_sem.at[slot]
            ).start()

    def wait_db(m):
        slot = lax.rem(m, DB)
        pltpu.make_async_copy(wd.at[0, :, cols(0)], db.at[slot], db_sem.at[slot]).wait()
        return slot

    start_gu(jnp.int32(0))
    for m in range(DB - 1):
        start_db(jnp.int32(m))

    barrier = pltpu.get_barrier_semaphore()
    for p in range(2):
        for d in range(1, S):
            pl.semaphore_signal(barrier, inc=1, device_id={"ep": dev(p, d, 0)})
    pl.semaphore_wait(barrier, 2 * (S - 1))

    def remote(src, dst, s, r, to):
        return pltpu.make_async_remote_copy(src, dst, s, r, device_id={"ep": to})

    def xcols(p):
        return x_ref.at[:, pl.ds(p * H, H)]

    def meta_copy(p, d):
        return remote(meta_ref, mall.at[p, S - d], m_s.at[p, d - 1], m_r.at[p, S - d - 1], dev(p, d, 0))

    def ag_first(p, d):
        i = 0 if d == 1 else 1
        return remote(xcols(p), ag.at[p, S - d - 1], ag_s.at[p, i], ag_r.at[p, i], dev(p, d, 0))

    def ag_relay(p, d):
        i = 0 if d == 1 else 1
        src = ag.at[p, (S - 1 if d == 1 else 1) - 1, pl.ds(i * HT, HT)]
        dst = ag.at[p, 2 - 1, pl.ds(i * HT, HT)]
        return remote(src, dst, ag_s.at[p, 2 + i], ag_r.at[p, 2 + i], dev(p, d, 0))

    for p in range(2):
        for d in range(1, S):
            meta_copy(p, d).start()
        for d in (1, S - 1):
            ag_first(p, d).start()
    for p in range(2):
        mall[p, 0] = meta_ref[...]

    def ffn_tile(lhs, rows, n, i):
        slot = wait_gu(n)
        start_gu(n + 1)
        g = dot(lhs, gu[slot, 0])
        u = dot(lhs, gu[slot, 1])
        h[0:rows, cols(i)] = (jax.nn.silu(g) * u).astype(BF16)

    for q in range(QS):

        def up(i, _):
            ffn_tile(x_ref[...], T, q * NG + i, i)
            return 0

        lax.fori_loop(0, NG, up, 0)

        def down(c, _):
            m = q * NDT + c
            slot = wait_db(m)
            start_db(m + DB - 1)
            o = dot(h[0:T, :], db[slot])
            ysh[:, cols(c)] = o if q == 0 else ysh[:, cols(c)] + o
            return 0

        lax.fori_loop(0, NDT, down, 0)

    for p in range(2):
        ag_first(p, 1).wait_recv()
        ag_relay(p, 1).start()
        ag_first(p, S - 1).wait_recv()
        ag_relay(p, S - 1).start()
    for p in range(2):
        for d in range(1, S):
            meta_copy(p, d).wait_recv()

    def source(p, r, c):
        if r == 0:
            return x_ref[:, pl.ds(pl.multiple_of(p * H + c * CT, CT), CT)]
        return ag[p, r - 1, :, cols(c)]

    def onehot(p, r):
        i = lax.broadcasted_iota(jnp.int32, (S * EPD * SL, T), 0)
        n = EPD * SL
        off = dev(p, 0, S - 1) * n - (S - 1) * n
        for k in range(S - 2, -1, -1):
            off = jnp.where(i < (k + 1) * n, (dev(p, 0, k) - k) * n, off)
        code = (i + off).astype(F32)
        total = jnp.zeros(code.shape, F32)
        for j in range(TOP):
            total += jnp.where(code == mall[p, r, j : j + 1, :], 1.0, 0.0)
        return total.astype(BF16)

    def select(p, pair):
        for j in range(2):
            oh[j] = onehot(p, 2 * pair + j)

        def tile(c, _):
            a = dot(oh[0], source(p, 2 * pair, c))
            b = dot(oh[1], source(p, 2 * pair + 1, c))
            for k in range(S):
                for e in range(EPD):
                    o = (k * EPD + e) * SL
                    lo = jnp.concatenate([a[o : o + LO], b[o : o + LO]], 0).astype(BF16)
                    hi = jnp.concatenate([a[o + LO : o + SL], b[o + LO : o + SL]], 0).astype(BF16)
                    l0, h0 = pair * 2 * LO, S * LO + pair * 2 * HI
                    if k == 0:
                        z[p, e, 0, l0 : l0 + 2 * LO, cols(c)] = lo
                        z[p, e, 0, h0 : h0 + 2 * HI, cols(c)] = hi
                    else:
                        dsend[p, k - 1, e * CH + l0 : e * CH + l0 + 2 * LO, cols(c)] = lo
                        dsend[p, k - 1, e * CH + h0 : e * CH + h0 + 2 * HI, cols(c)] = hi
            return 0

        lax.fori_loop(0, HTILES, tile, 0)

    for p in range(2):
        select(p, 0)
    for p in range(2):
        for d in (1, S - 1):
            ag_relay(p, d).wait_recv()
    for p in range(2):
        select(p, 1)

    def z_copy(p, e, k):
        rows = pl.ds(e * CH, CH) if isinstance(e, int) else pl.ds(pl.multiple_of(e * CH, CH), CH)
        return remote(
            dsend.at[p, k - 1, rows], z.at[p, e, S - k],
            z_s.at[p, e, k - 1], z_r.at[p, e, S - k - 1], dev(p, 0, k),
        )

    for e in range(EPD):
        for k in (1, S - 1, 2):
            for p in range(2):
                z_copy(p, e, k).start()

    def coefficients(n, _):
        p, r = lax.div(n, S), lax.rem(n, S)
        half = EPD * S * LO
        i = lax.broadcasted_iota(jnp.int32, (2 * half, T), 0)
        high = i >= half
        i = jnp.where(high, i - half, i)
        e, kk, c = i >> 6, (i >> 4) & 3, i & 15
        owner = jnp.where(kk == 0, dev(p, 0, 0), 0)
        for k in range(1, S):
            owner = jnp.where(kk == k, dev(p, 0, k), owner)
        odd = c >> 3
        slot = jnp.where(high, LO + (c & 7), c)
        code = (owner * EPD + e) * SL + slot
        code = jnp.where(jnp.logical_and(high, odd != lax.rem(r, 2)), -2, code).astype(F32)
        total = jnp.zeros(code.shape, F32)
        for j in range(TOP):
            total += jnp.where(code == mall[p, r, j : j + 1, :], mall[p, r, 8 + j : 9 + j, :], 0.0)
        cmat[p, r] = total.T.astype(BF16)
        return 0

    lax.fori_loop(0, 2 * S, coefficients, 0)

    def c_copy(p, e, k):
        return remote(
            z.at[p, e, k], crecv.at[p, e, S - k],
            c_s.at[p, e, k - 1], c_r.at[p, e, S - k - 1], dev(p, 0, k),
        )

    def expert(e, _):
        for k in (1, S - 1, 2):
            for p in range(2):
                z_copy(p, e, k).wait_recv()
        for k in range(S):
            zf[k * CH : (k + 1) * CH, 0:H] = z[0, e, k]
            for r in range(S):
                o = k * CH + r * LO
                zf[o : o + LO, H:D] = z[1, e, r, k * LO : (k + 1) * LO]
            u0 = S * LO + (k // 2) * 2 * HI
            for r in range(0, S, 2):
                o = k * CH + S * LO + r * HI
                part = [
                    z[1, e, r + j, u0 : u0 + 2 * HI].astype(F32)[(k % 2) * HI : (k % 2 + 1) * HI]
                    for j in range(2)
                ]
                zf[o : o + 2 * HI, H:D] = jnp.concatenate(part, 0).astype(BF16)

        def up(i, _):
            ffn_tile(zf[...], S * CH, (QS + e) * NG + i, i)
            return 0

        lax.fori_loop(0, NG, up, 0)

        for p in range(2):

            def down(c, _):
                m = (QS + e) * NDT + p * HTILES + c
                slot = wait_db(m)
                start_db(m + DB - 1)
                o = dot(h[...], db[slot])
                for k in range(S):
                    if p == 0:
                        b = o[k * CH : (k + 1) * CH]
                    else:
                        low = [o[r * CH + k * LO : r * CH + (k + 1) * LO] for r in range(S)]
                        n = S * LO + k * HI
                        high = [o[r * CH + n : r * CH + n + HI] for r in range(S)]
                        b = jnp.concatenate(low + high, 0)
                    if k == 0:
                        crecv[p, e, 0, :, cols(c)] = b.astype(BF16)
                    else:
                        z[p, e, k, :, cols(c)] = b.astype(BF16)
                return 0

            lax.fori_loop(0, HTILES, down, 0)
            for k in (1, S - 1, 2):
                c_copy(p, e, k).start()
        return 0

    lax.fori_loop(0, EPD, expert, 0)

    for p in range(2):
        for e in range(EPD):
            for k in range(1, S):
                z_copy(p, e, k).wait_send()

    def slots(p, r, c):
        a = crecv[p, :, :, r * LO : (r + 1) * LO, cols(c)].reshape(EPD * S * LO, CT)
        u0 = S * LO + (r // 2) * 2 * HI
        b = crecv[p, :, :, u0 : u0 + 2 * HI, cols(c)].reshape(EPD * S * LO, CT)
        return jnp.concatenate([a, b], 0)

    def part(p, r, c, r0, r1):
        return dot(cmat[p, r, r0:r1], slots(p, r, c))

    def via_copy(p, i):
        src = dsend.at[p, 1, pl.ds(i * HT, HT)]
        return remote(src, via.at[p, i], v_s.at[p, i], v_r.at[p, i], dev(p, 1 if i == 0 else S - 1, 0))

    def fin_copy(p, i, half):
        src = dsend.at[p, 2 * i, pl.ds(half * HT, HT)]
        dst = fin.at[p, i, pl.ds(half * HT, HT)]
        return remote(src, dst, f_s.at[p, i, half], f_r.at[p, i, half], dev(p, 1 if i == 0 else S - 1, 0))

    for p in range(2):
        for e in range(EPD):
            for k in range(1, S):
                c_copy(p, e, k).wait_recv()

        def far(c, _):
            dsend[p, 1, 0:T, cols(c)] = part(p, 2, c, 0, T).astype(BF16)
            return 0

        lax.fori_loop(0, HTILES, far, 0)
        for i in range(2):
            via_copy(p, i).start()

    for p in range(2):

        def near(c, _):
            dsend[p, 0, HT:T, cols(c)] = part(p, 1, c, HT, T).astype(BF16)
            dsend[p, 2, 0:HT, cols(c)] = part(p, S - 1, c, 0, HT).astype(BF16)
            return 0

        lax.fori_loop(0, HTILES, near, 0)
        fin_copy(p, 0, 1).start()
        fin_copy(p, 1, 0).start()

    for p in range(2):
        for i in range(2):
            via_copy(p, i).wait_recv()

        def through(c, _):
            a = part(p, 1, c, 0, HT) + via[p, 0, :, cols(c)].astype(F32)
            b = part(p, S - 1, c, HT, T) + via[p, 1, :, cols(c)].astype(F32)
            dsend[p, 0, 0:HT, cols(c)] = a.astype(BF16)
            dsend[p, 2, HT:T, cols(c)] = b.astype(BF16)
            return 0

        lax.fori_loop(0, HTILES, through, 0)
        fin_copy(p, 0, 0).start()
        fin_copy(p, 1, 1).start()

    for p in range(2):

        def own(c, _):
            ysh[:, cols(p * HTILES + c)] += part(p, 0, c, 0, T)
            return 0

        lax.fori_loop(0, HTILES, own, 0)

    for p in range(2):
        for i in range(2):
            for half in range(2):
                fin_copy(p, i, half).wait_recv()

        def last(c, _):
            a = fin[p, 0, :, cols(c)].astype(F32) + fin[p, 1, :, cols(c)].astype(F32)
            at = cols(p * HTILES + c)
            y_ref[:, at] = (ysh[:, at] + a).astype(y_ref.dtype)
            return 0

        lax.fori_loop(0, HTILES, last, 0)

    for p in range(2):
        for d in range(1, S):
            meta_copy(p, d).wait_send()
        for d in (1, S - 1):
            ag_first(p, d).wait_send()
            ag_relay(p, d).wait_send()
        for e in range(EPD):
            for k in range(1, S):
                c_copy(p, e, k).wait_send()
        for i in range(2):
            via_copy(p, i).wait_send()
            for half in range(2):
                fin_copy(p, i, half).wait_send()


def solution(mesh):
    side = math.isqrt(mesh.shape["ep"])

    def local(x, expert, slot, gate, w_gate, w_up, w_down, s_gate, s_up, s_down):
        T, D = x.shape[2:]
        TOP = expert.shape[3]
        EPD, _, FF = w_gate.shape
        SL, S, H = LO + HI, side, D // 2
        assert side * side == mesh.shape["ep"] and side == 4
        assert SL == 5 * T * TOP // (4 * EPD * mesh.shape["ep"])
        code = jnp.where(slot < SL, expert * SL + slot, -1).astype(F32).reshape(T, TOP)
        meta = jnp.pad(
            jnp.stack([code.T, gate.reshape(T, TOP).T]), ((0, 0), (0, 8 - TOP), (0, 0))
        ).reshape(16, T)
        rows = EPD * S * SL
        sem = pltpu.SemaphoreType.DMA
        y = pl.pallas_call(
            functools.partial(kernel, S, EPD, TOP),
            out_shape=jax.ShapeDtypeStruct((T, D), x.dtype),
            in_specs=[pl.BlockSpec(memory_space=pltpu.VMEM)] * 2
            + [pl.BlockSpec(memory_space=pl.ANY)] * 6,
            out_specs=pl.BlockSpec(memory_space=pltpu.VMEM),
            scratch_shapes=[
                pltpu.VMEM((2, S - 1, T, H), BF16),
                pltpu.VMEM((2, S, 16, T), F32),
                pltpu.VMEM((2, rows, T), BF16),
                pltpu.VMEM((2, S - 1, rows, H), BF16),
                pltpu.VMEM((2, EPD, S, S * SL, H), BF16),
                pltpu.VMEM((S * S * SL, D), BF16),
                pltpu.VMEM((2, EPD, S, S * SL, H), BF16),
                pltpu.VMEM((2, 2, T // 2, H), BF16),
                pltpu.VMEM((2, 2, T, H), BF16),
                pltpu.VMEM((2, S, T, 2 * EPD * S * LO), BF16),
                pltpu.VMEM((S * S * SL, FF), BF16),
                pltpu.VMEM((T, D), F32),
                pltpu.VMEM((2, 2, D, CT), BF16),
                pltpu.VMEM((DB, FF, CT), BF16),
                sem((2, 2)), sem((DB,)),
                sem((2, 4)), sem((2, 4)),
                sem((2, S - 1)), sem((2, S - 1)),
                sem((2, EPD, S - 1)), sem((2, EPD, S - 1)),
                sem((2, EPD, S - 1)), sem((2, EPD, S - 1)),
                sem((2, 2)), sem((2, 2)),
                sem((2, 2, 2)), sem((2, 2, 2)),
            ],
            compiler_params=pltpu.CompilerParams(
                collective_id=0, has_side_effects=True, vmem_limit_bytes=67043328
            ),
        )(x.reshape(T, D), meta, w_gate, w_up, w_down, s_gate, s_up, s_down)
        return y.reshape(x.shape)

    own, experts, whole = P("dp", "ep"), P("ep"), P()
    return jax.shard_map(
        local,
        mesh=mesh,
        in_specs=(own,) * 4 + (experts,) * 3 + (whole,) * 3,
        out_specs=own,
        check_vma=False,
    )
```

time: 405 us -> 189 us (0.47)
  Pallas kernels: 0 us -> 183 us
  matrix products: 133 us -> 0 us
  blocking collectives: 128 us -> 0 us
  waiting for transfers between devices: 118 us -> 0 us
  local copies, waits for them, and re-layouts: 15.7 us -> 3.15 us
  starting transfers between devices: 5.54 us -> 0 us
    pallas_call x0 -> x1, Pallas kernels: none -> 183 us  [local(): pl.pallas_call(functools.partial(kernel, S, EPD, TOP), out_shape=jax.Shap...]
    dot_general x10 -> x0, matrix products: 133 us -> none  [einsum(): return jnp.einsum(form, a.astype(jnp.float32), b.astype(jnp.float32))]
    another operation x1 -> x0, blocking collectives: 128 us -> none  [placed(): return lax.with_sharding_constraint(v, NamedSharding(mesh, P(*spec)))]
    another operation x1 -> x0, waiting for transfers between devices: 118 us -> none  [placed(): return lax.with_sharding_constraint(v, NamedSharding(mesh, P(*spec)))]
    another operation x1 -> x0, local copies, waits for them, and re-layouts: 8.24 us -> none  [placed(): return lax.with_sharding_constraint(v, NamedSharding(mesh, P(*spec)))]
    another operation x1 -> x0, starting transfers between devices: 5.54 us -> none  [placed(): return lax.with_sharding_constraint(v, NamedSharding(mesh, P(*spec)))]
    convert_element_type x3 -> x0, local copies, waits for them, and re-layouts: 5.04 us -> none  [the longest x1 2.45 us: step(): einsum('abtke,abtkc->abtec', to_expert, to_slot).astype(jnp.bfloat16)]
  transfers between devices with their start and end apart: 1 -> 0, of which waited for: 1 -> 0; matrix products, arithmetic and copies ran while one was open for 6% -> 0% of each run, Pallas kernels for 0% -> 0%
where the time goes in v1:
time: 189 us; the launch traced here: 188 us
  Pallas kernels  183 us (97%)
  local copies, waits for them, and re-layouts  3.15 us (2%)
    pallas_call x1, Pallas kernels, local(): pl.pallas_call(functools.partial(kernel, S, EPD, TOP), out_shape=jax.Shap...  183 us

profile of v1, /device:TPU:96, one launch (start us, length us, event | category | flops | bytes accessed | tf_op | source)
XLA Modules:
  0.0 187.6 jit_solution(3351475206780644063)
XLA Ops:
  0.0 0.7 fusion.3
  0.7 0.7 copy.29
  1.4 0.6 fusion.meta_ref
  2.0 183.1 %shard_map.100 = bf16[256,2560]{1,0:T(8,128)(2,1)} custom-call(bf16[256,2560]{1,0:T(8,128)(2,1)} %bitcast.18, f32[16,256]{1,0:T(8,128)} %fusion.meta_ref, bf16[5,2560,1536]{2,1,0:T(8,128)(2,1)} %wg.1, bf16[5,2560,1536]{2,1,0:T(8,128)(2,1)} %wu.1, bf16[5,1536,2560]{2,1,0:T(8,128)(2,1)} %wd.1, bf16[2560,3072]{1,0:T(8,128)(2,1)} %sg.1, bf16[2560,3072]{1,0:T(8,128)(2,1)} %su.1, ...), custom_call_target="tpu_custom_call" | custom-call | tf_op jit(solution)/shard_map/pallas_call | solution.py:416
  185.2 2.5 %copy.31 = bf16[1,1,256,2560]{3,2,1,0:T(8,128)(2,1)} copy(bf16[1,1,256,2560]{3,2,1,0:T(8,128)(2,1)} %bitcast.17) | data formatting | bytes 2621440

commit v2 on v1

v2 whole, which is shorter than its diff:
```python
import functools
import math

import jax
import jax.numpy as jnp
from jax import lax
from jax.experimental import pallas as pl
from jax.experimental.pallas import tpu as pltpu
from jax.sharding import PartitionSpec as P

F32, BF16 = jnp.float32, jnp.bfloat16
LO, HI = 16, 8
CT = 256
DB = 4
EARLY = 1


def dot(a, b):
    return jnp.dot(a, b, preferred_element_type=F32)


def cols(i):
    return pl.ds(pl.multiple_of(i * CT, CT), CT)


def kernel(
    S, EPD, TOP,
    x_hbm, expert_ref, slot_ref, gate_ref, wg, wu, wd, sg, su, sd, y_ref,
    x_ref, meta_ref, flip, ag, mall, oh, dsend, z, zf, crecv, via, fin, cmat, h, ysh, gu, db,
    x_sem, gu_sem, db_sem, ag_s, ag_r, m_s, m_r, z_s, z_r, c_s, c_r, v_s, v_r, f_s, f_r,
):
    T, D = x_ref.shape
    FF = wg.shape[2]
    H = D // 2
    SL = LO + HI
    CH = S * SL
    HT = T // 2
    PR = 2 * SL
    LAST = EPD + 1
    NG, NDT = FF // CT, D // CT
    HTILES = H // CT
    me = lax.axis_index("ep")
    px, py = lax.div(me, S), lax.rem(me, S)

    def dev(p, df, ds):
        dx = df * (1 - p) + ds * p
        dy = df * p + ds * (1 - p)
        return lax.rem(px + dx, S) * S + lax.rem(py + dy, S)

    def lo(r):
        return (r // 2) * PR + (r % 2) * LO

    def hi(r):
        return (r // 2) * PR + 2 * LO + (r % 2) * HI

    def start_gu(n):
        slot = lax.rem(n, 2)
        u, c = lax.div(n, NG), lax.rem(n, NG)

        @pl.when(jnp.logical_or(u == 0, u == LAST))
        def _():
            at = cols(c + lax.div(u, LAST) * NG)
            pltpu.make_async_copy(sg.at[:, at], gu.at[slot, 0], gu_sem.at[slot, 0]).start()
            pltpu.make_async_copy(su.at[:, at], gu.at[slot, 1], gu_sem.at[slot, 1]).start()

        @pl.when(jnp.logical_and(u > 0, u < LAST))
        def _():
            pltpu.make_async_copy(wg.at[u - 1, :, cols(c)], gu.at[slot, 0], gu_sem.at[slot, 0]).start()
            pltpu.make_async_copy(wu.at[u - 1, :, cols(c)], gu.at[slot, 1], gu_sem.at[slot, 1]).start()

    def wait_gu(n):
        slot = lax.rem(n, 2)
        for j in range(2):
            pltpu.make_async_copy(sg.at[:, cols(0)], gu.at[slot, j], gu_sem.at[slot, j]).wait()
        return slot

    def start_db(m):
        slot = lax.rem(m, DB)
        u, c = lax.div(m, NDT), lax.rem(m, NDT)

        @pl.when(jnp.logical_or(u == 0, u == LAST))
        def _():
            rows = pl.ds(pl.multiple_of(lax.div(u, LAST) * FF, FF), FF)
            pltpu.make_async_copy(sd.at[rows, cols(c)], db.at[slot], db_sem.at[slot]).start()

        @pl.when(jnp.logical_and(u > 0, u < LAST))
        def _():
            pltpu.make_async_copy(wd.at[u - 1, :, cols(c)], db.at[slot], db_sem.at[slot]).start()

    def wait_db(m):
        slot = lax.rem(m, DB)
        pltpu.make_async_copy(wd.at[0, :, cols(0)], db.at[slot], db_sem.at[slot]).wait()
        return slot

    x_copy = pltpu.make_async_copy(x_hbm, x_ref, x_sem)
    x_copy.start()
    start_gu(jnp.int32(0))
    for m in range(DB - 1):
        start_db(jnp.int32(m))

    barrier = pltpu.get_barrier_semaphore()
    for p in range(2):
        for d in range(1, S):
            pl.semaphore_signal(barrier, inc=1, device_id={"ep": dev(p, d, 0)})
    pl.semaphore_wait(barrier, 2 * (S - 1))

    def remote(src, dst, s, r, to):
        return pltpu.make_async_remote_copy(src, dst, s, r, device_id={"ep": to})

    def ag_first(p, d, early):
        i = 0 if d == 1 else 1
        rows = pl.ds((i if early else 1 - i) * HT, HT)
        n = i if early else 2 + i
        return remote(
            x_hbm.at[rows, pl.ds(p * H, H)], ag.at[p, S - d - 1, rows],
            ag_s.at[p, n], ag_r.at[p, n], dev(p, d, 0),
        )

    def ag_relay(p, d):
        i = 0 if d == 1 else 1
        rows = pl.ds(i * HT, HT)
        src = ag.at[p, (S - 1 if d == 1 else 1) - 1, rows]
        return remote(src, ag.at[p, 1, rows], ag_s.at[p, 4 + i], ag_r.at[p, 4 + i], dev(p, d, 0))

    def meta_copy(p, d):
        return remote(meta_ref, mall.at[p, S - d], m_s.at[p, d - 1], m_r.at[p, S - d - 1], dev(p, d, 0))

    for early in (True, False):
        for p in range(2):
            for d in (1, S - 1):
                ag_first(p, d, early).start()

    flip[...] = jnp.zeros(flip.shape, F32)
    slot = slot_ref[...]
    flip[0, :, 0:TOP] = jnp.where(slot < SL, expert_ref[...] * SL + slot, -1).astype(F32)
    flip[1, :, 0:TOP] = gate_ref[...]
    meta_ref[0:8] = flip[0].T[0:8]
    meta_ref[8:16] = flip[1].T[0:8]
    for p in range(2):
        mall[p, 0] = meta_ref[...]
        for d in range(1, S):
            meta_copy(p, d).start()

    def up(lhs, rows, u):
        def tile(i, _):
            n = u * NG + i
            slot = wait_gu(n)
            pl.when(n + 1 < (LAST + 1) * NG)(lambda: start_gu(n + 1))
            g = dot(lhs[...], gu[slot, 0])
            v = dot(lhs[...], gu[slot, 1])
            h[0:rows, cols(i)] = (jax.nn.silu(g) * v).astype(BF16)
            return 0

        lax.fori_loop(0, NG, tile, 0)

    def down_tile(rows, u, c):
        m = u * NDT + c
        slot = wait_db(m)
        pl.when(m + DB - 1 < (LAST + 1) * NDT)(lambda: start_db(m + DB - 1))
        return dot(h[0:rows, :], db[slot])

    def shared_down(u):
        def tile(c, _):
            o = down_tile(T, u, c)
            ysh[:, cols(c)] = o if u == 0 else ysh[:, cols(c)] + o
            return 0

        lax.fori_loop(0, NDT, tile, 0)

    x_copy.wait()
    up(x_ref, T, 0)
    for p in range(2):
        for d in (1, S - 1):
            ag_first(p, d, True).wait_recv()
        ag_relay(p, 1).start()
        ag_relay(p, S - 1).start()
    shared_down(0)

    for p in range(2):
        for d in (1, S - 1):
            ag_first(p, d, False).wait_recv()
        for d in range(1, S):
            meta_copy(p, d).wait_recv()

    def source(p, r, c):
        if r == 0:
            return x_ref[:, pl.ds(pl.multiple_of(p * H + c * CT, CT), CT)]
        return ag[p, r - 1, :, cols(c)]

    def onehot(p, r):
        i = lax.broadcasted_iota(jnp.int32, (S * EPD * SL, T), 0)
        n = EPD * SL
        off = dev(p, 0, S - 1) * n - (S - 1) * n
        for k in range(S - 2, -1, -1):
            off = jnp.where(i < (k + 1) * n, (dev(p, 0, k) - k) * n, off)
        code = (i + off).astype(F32)
        total = jnp.zeros(code.shape, F32)
        for j in range(TOP):
            total += jnp.where(code == mall[p, r, j : j + 1, :], 1.0, 0.0)
        return total.astype(BF16)

    def select(p, pair):
        for j in range(2):
            oh[j] = onehot(p, 2 * pair + j)

        def tile(c, _):
            a = dot(oh[0], source(p, 2 * pair, c))
            b = dot(oh[1], source(p, 2 * pair + 1, c))
            for k in range(S):
                for e in range(EPD):
                    o = (k * EPD + e) * SL
                    m = o + LO
                    b48 = jnp.concatenate([a[o:m], b[o:m], a[m : o + SL], b[m : o + SL]], 0)
                    at = pair * PR
                    if k == 0:
                        z[p, e, 0, at : at + PR, cols(c)] = b48.astype(BF16)
                    else:
                        at += e * CH
                        dsend[p, k - 1, at : at + PR, cols(c)] = b48.astype(BF16)
            return 0

        lax.fori_loop(0, HTILES, tile, 0)

    def halves(e):
        return (0, 1) if e < EARLY else (2,)

    def z_copy(p, e, k, half):
        at, n = (half * PR, PR) if half < 2 else (0, CH)
        rows = pl.ds(pl.multiple_of(e * CH + at, PR), n)
        return remote(
            dsend.at[p, k - 1, rows], z.at[p, e, S - k, pl.ds(at, n)],
            z_s.at[p, e, k - 1, half % 2], z_r.at[p, e, S - k - 1, half % 2], dev(p, 0, k),
        )

    def z_start(e, half):
        for k in (1, S - 1, 2):
            for p in range(2):
                z_copy(p, e, k, half).start()

    for p in range(2):
        select(p, 0)
    for e in range(EARLY):
        z_start(e, 0)
    for p in range(2):
        for d in (1, S - 1):
            ag_relay(p, d).wait_recv()
    for p in range(2):
        select(p, 1)
    for e in range(EPD):
        z_start(e, 1 if e < EARLY else 2)

    def coefficients(n, _):
        p, r = lax.div(n, S), lax.rem(n, S)
        half = EPD * S * LO
        i = lax.broadcasted_iota(jnp.int32, (2 * half, T), 0)
        high = i >= half
        i = jnp.where(high, i - half, i)
        e, kk, c = i >> 6, (i >> 4) & 3, i & 15
        owner = jnp.where(kk == 0, dev(p, 0, 0), 0)
        for k in range(1, S):
            owner = jnp.where(kk == k, dev(p, 0, k), owner)
        odd = c >> 3
        slot = jnp.where(high, LO + (c & 7), c)
        code = (owner * EPD + e) * SL + slot
        code = jnp.where(jnp.logical_and(high, odd != lax.rem(r, 2)), -2, code).astype(F32)
        total = jnp.zeros(code.shape, F32)
        for j in range(TOP):
            total += jnp.where(code == mall[p, r, j : j + 1, :], mall[p, r, 8 + j : 9 + j, :], 0.0)
        cmat[p, r] = total.T.astype(BF16)
        return 0

    lax.fori_loop(0, 2 * S, coefficients, 0)

    def c_copy(p, e, k, half):
        at, n = (half * PR, PR) if half < 2 else (0, CH)
        return remote(
            z.at[p, e, k, pl.ds(at, n)], crecv.at[p, e, S - k, pl.ds(at, n)],
            c_s.at[p, e, k - 1, half % 2], c_r.at[p, e, S - k - 1, half % 2], dev(p, 0, k),
        )

    def expert(e, _):
        def arrived(half):
            for k in (1, S - 1, 2):
                for p in range(2):
                    z_copy(p, e, k, half).wait_recv()

        @pl.when(e < EARLY)
        def _():
            arrived(0)
            arrived(1)

        @pl.when(e >= EARLY)
        def _():
            arrived(2)

        for k in range(S):
            zf[k * CH : (k + 1) * CH, 0:H] = z[0, e, k]
            for r in range(S):
                o = k * CH + lo(r)
                zf[o : o + LO, H:D] = z[1, e, r, lo(k) : lo(k) + LO]
            u0 = hi(k) - (k % 2) * HI
            for r in range(0, S, 2):
                o = k * CH + hi(r)
                two = [
                    z[1, e, r + j, u0 : u0 + 2 * HI].astype(F32)[(k % 2) * HI : (k % 2 + 1) * HI]
                    for j in range(2)
                ]
                zf[o : o + 2 * HI, H:D] = jnp.concatenate(two, 0).astype(BF16)

        up(zf, S * CH, 1 + e)

        def back(p, half):
            for k in (1, S - 1, 2):
                c_copy(p, e, k, half).start()

        for p in range(2):

            def tile(c, _):
                o = down_tile(S * CH, 1 + e, p * HTILES + c)
                for k in range(S):
                    if p == 0:
                        b = o[k * CH : (k + 1) * CH]
                    else:
                        rows = []
                        for r in range(0, S, 2):
                            for f, n in ((lo(k), LO), (hi(k), HI)):
                                rows += [o[q * CH + f : q * CH + f + n] for q in (r, r + 1)]
                        b = jnp.concatenate(rows, 0)
                    if k == 0:
                        crecv[p, e, 0, :, cols(c)] = b.astype(BF16)
                    else:
                        z[p, e, k, :, cols(c)] = b.astype(BF16)
                return 0

            lax.fori_loop(0, HTILES, tile, 0)
            pl.when(e < EPD - 1)(lambda: back(p, 2))

        @pl.when(e == EPD - 1)
        def _():
            for half in (1, 0):
                for p in range(2):
                    back(p, half)

        return 0

    lax.fori_loop(0, EPD, expert, 0)
    up(x_ref, T, LAST)
    shared_down(LAST)

    for p in range(2):
        for e in range(EPD):
            for k in range(1, S):
                for half in halves(e):
                    z_copy(p, e, k, half).wait_send()

    def slots(p, r, c):
        a = crecv[p, :, :, lo(r) : lo(r) + LO, cols(c)].reshape(EPD * S * LO, CT)
        u0 = hi(r) - (r % 2) * HI
        b = crecv[p, :, :, u0 : u0 + 2 * HI, cols(c)].reshape(EPD * S * LO, CT)
        return jnp.concatenate([a, b], 0)

    def part(p, r, c, r0, r1):
        return dot(cmat[p, r, r0:r1], slots(p, r, c))

    def via_copy(p, i):
        src = dsend.at[p, 1, pl.ds(i * HT, HT)]
        return remote(src, via.at[p, i], v_s.at[p, i], v_r.at[p, i], dev(p, 1 if i == 0 else S - 1, 0))

    def fin_copy(p, i, half):
        src = dsend.at[p, 2 * i, pl.ds(half * HT, HT)]
        dst = fin.at[p, i, pl.ds(half * HT, HT)]
        return remote(src, dst, f_s.at[p, i, half], f_r.at[p, i, half], dev(p, 1 if i == 0 else S - 1, 0))

    for p in range(2):
        for e in range(EPD):
            for k in range(1, S):
                c_copy(p, e, k, 2 if e < EPD - 1 else 1).wait_recv()

        def far(c, _):
            dsend[p, 1, 0:T, cols(c)] = part(p, 2, c, 0, T).astype(BF16)
            return 0

        lax.fori_loop(0, HTILES, far, 0)
        for i in range(2):
            via_copy(p, i).start()

    for p in range(2):

        def before(c, _):
            dsend[p, 2, 0:HT, cols(c)] = part(p, S - 1, c, 0, HT).astype(BF16)
            return 0

        lax.fori_loop(0, HTILES, before, 0)
        fin_copy(p, 1, 0).start()

    for p in range(2):
        for k in range(1, S):
            c_copy(p, EPD - 1, k, 0).wait_recv()

        def after(c, _):
            dsend[p, 0, HT:T, cols(c)] = part(p, 1, c, HT, T).astype(BF16)
            return 0

        lax.fori_loop(0, HTILES, after, 0)
        fin_copy(p, 0, 1).start()

    for p in range(2):
        for i in range(2):
            via_copy(p, i).wait_recv()

        def through(c, _):
            a = part(p, 1, c, 0, HT) + via[p, 0, :, cols(c)].astype(F32)
            b = part(p, S - 1, c, HT, T) + via[p, 1, :, cols(c)].astype(F32)
            dsend[p, 0, 0:HT, cols(c)] = a.astype(BF16)
            dsend[p, 2, HT:T, cols(c)] = b.astype(BF16)
            return 0

        lax.fori_loop(0, HTILES, through, 0)
        fin_copy(p, 0, 0).start()
        fin_copy(p, 1, 1).start()

    for p in range(2):

        def own(c, _):
            ysh[:, cols(p * HTILES + c)] += part(p, 0, c, 0, T)
            return 0

        lax.fori_loop(0, HTILES, own, 0)

    for p in range(2):
        for i in range(2):
            for half in range(2):
                fin_copy(p, i, half).wait_recv()

        def last(c, _):
            a = fin[p, 0, :, cols(c)].astype(F32) + fin[p, 1, :, cols(c)].astype(F32)
            at = cols(p * HTILES + c)
            y_ref[:, at] = (ysh[:, at] + a).astype(y_ref.dtype)
            return 0

        lax.fori_loop(0, HTILES, last, 0)

    for p in range(2):
        for d in range(1, S):
            meta_copy(p, d).wait_send()
        for d in (1, S - 1):
            for early in (True, False):
                ag_first(p, d, early).wait_send()
            ag_relay(p, d).wait_send()
        for e in range(EPD):
            for k in range(1, S):
                for half in (2,) if e < EPD - 1 else (0, 1):
                    c_copy(p, e, k, half).wait_send()
        for i in range(2):
            via_copy(p, i).wait_send()
            for half in range(2):
                fin_copy(p, i, half).wait_send()


def solution(mesh):
    side = math.isqrt(mesh.shape["ep"])

    def local(x, expert, slot, gate, w_gate, w_up, w_down, s_gate, s_up, s_down):
        T, D = x.shape[2:]
        TOP = expert.shape[3]
        EPD, _, FF = w_gate.shape
        SL, S, H = LO + HI, side, D // 2
        assert side * side == mesh.shape["ep"] and side == 4
        assert FF * 2 == s_gate.shape[1] and SL == 5 * T * TOP // (4 * EPD * mesh.shape["ep"])
        rows = EPD * S * SL
        sem = pltpu.SemaphoreType.DMA
        y = pl.pallas_call(
            functools.partial(kernel, S, EPD, TOP),
            out_shape=jax.ShapeDtypeStruct((T, D), x.dtype),
            in_specs=[pl.BlockSpec(memory_space=pl.ANY)]
            + [pl.BlockSpec(memory_space=pltpu.VMEM)] * 3
            + [pl.BlockSpec(memory_space=pl.ANY)] * 6,
            out_specs=pl.BlockSpec(memory_space=pltpu.VMEM),
            scratch_shapes=[
                pltpu.VMEM((T, D), BF16),
                pltpu.VMEM((16, T), F32),
                pltpu.VMEM((2, T, 128), F32),
                pltpu.VMEM((2, S - 1, T, H), BF16),
                pltpu.VMEM((2, S, 16, T), F32),
                pltpu.VMEM((2, rows, T), BF16),
                pltpu.VMEM((2, S - 1, rows, H), BF16),
                pltpu.VMEM((2, EPD, S, S * SL, H), BF16),
                pltpu.VMEM((S * S * SL, D), BF16),
                pltpu.VMEM((2, EPD, S, S * SL, H), BF16),
                pltpu.VMEM((2, 2, T // 2, H), BF16),
                pltpu.VMEM((2, 2, T, H), BF16),
                pltpu.VMEM((2, S, T, 2 * EPD * S * LO), BF16),
                pltpu.VMEM((S * S * SL, FF), BF16),
                pltpu.VMEM((T, D), F32),
                pltpu.VMEM((2, 2, D, CT), BF16),
                pltpu.VMEM((DB, FF, CT), BF16),
                sem, sem((2, 2)), sem((DB,)),
                sem((2, 6)), sem((2, 6)),
                sem((2, S - 1)), sem((2, S - 1)),
                sem((2, EPD, S - 1, 2)), sem((2, EPD, S - 1, 2)),
                sem((2, EPD, S - 1, 2)), sem((2, EPD, S - 1, 2)),
                sem((2, 2)), sem((2, 2)),
                sem((2, 2, 2)), sem((2, 2, 2)),
            ],
            compiler_params=pltpu.CompilerParams(
                collective_id=0, has_side_effects=True, vmem_limit_bytes=67043328
            ),
        )(x.reshape(T, D), *(v.reshape(T, TOP) for v in (expert, slot, gate)), w_gate, w_up, w_down, s_gate, s_up, s_down)
        return y.reshape(x.shape)

    own, experts, whole = P("dp", "ep"), P("ep"), P()
    return jax.shard_map(
        local,
        mesh=mesh,
        in_specs=(own,) * 4 + (experts,) * 3 + (whole,) * 3,
        out_specs=own,
        check_vma=False,
    )
```

time: 189 us -> 170 us (0.90)
  Pallas kernels: 183 us -> 162 us
  local copies, waits for them, and re-layouts: 3.15 us -> 6.9 us
    pallas_call x1, Pallas kernels: 183 us -> 162 us  [local(): pl.pallas_call(functools.partial(kernel, S, EPD, TOP), out_shape=jax.Shap...]
    unnamed x2 -> x4, local copies, waits for them, and re-layouts: 3.15 us -> 6.9 us
where the time goes in v2:
time: 170 us; the launch traced here: 168 us
  Pallas kernels  162 us (95%)
  local copies, waits for them, and re-layouts  6.9 us (4%)
    pallas_call x1, Pallas kernels, local(): pl.pallas_call(functools.partial(kernel, S, EPD, TOP), out_shape=jax.Shap...  162 us
    unnamed x4, local copies, waits for them, and re-layouts  6.9 us

profile of v2, /device:TPU:96, one launch (start us, length us, event | category | flops | bytes accessed | tf_op | source)
XLA Modules:
  0.0 168.4 jit_solution(11205158634204539135)
XLA Ops:
  0.0 1.5 copy.11
  1.5 1.5 copy.12
  3.0 1.5 copy.13
  4.4 161.5 %shard_map.100 = bf16[256,2560]{1,0:T(8,128)(2,1)} custom-call(bf16[256,2560]{1,0:T(8,128)(2,1)} %bitcast.6, s32[256,6]{1,0:T(8,128)} %bitcast.7, s32[256,6]{1,0:T(8,128)} %bitcast.8, f32[256,6]{1,0:T(8,128)} %bitcast.9, bf16[5,2560,1536]{2,1,0:T(8,128)(2,1)} %wg.1, bf16[5,2560,1536]{2,1,0:T(8,128)(2,1)} %wu.1, bf16[5,1536,2560]{2,1,0:T(8,128)(2,1)} %wd.1, ...), custom_call_target="tpu_custom_call" | custom-call | tf_op jit(solution)/shard_map/pallas_call | solution.py:472
  166.0 2.5 %copy.15 = bf16[1,1,256,2560]{3,2,1,0:T(8,128)(2,1)} copy(bf16[1,1,256,2560]{3,2,1,0:T(8,128)(2,1)} %bitcast.5) | data formatting | bytes 2621440

commit v3 on v2

--- a/solution.py
+++ b/solution.py
@@ -26,7 +26,7 @@
 def kernel(
     S, EPD, TOP,
     x_hbm, expert_ref, slot_ref, gate_ref, wg, wu, wd, sg, su, sd, y_ref,
-    x_ref, meta_ref, flip, ag, mall, oh, dsend, z, zf, crecv, via, fin, cmat, h, ysh, gu, db,
+    x_ref, meta_ref, ag, mall, oh, dsend, z, zf, crecv, via, fin, cmat, h, ysh, gu, db,
     x_sem, gu_sem, db_sem, ag_s, ag_r, m_s, m_r, z_s, z_r, c_s, c_r, v_s, v_r, f_s, f_r,
 ):
     T, D = x_ref.shape
@@ -130,12 +130,11 @@
             for d in (1, S - 1):
                 ag_first(p, d, early).start()
 
-    flip[...] = jnp.zeros(flip.shape, F32)
-    slot = slot_ref[...]
-    flip[0, :, 0:TOP] = jnp.where(slot < SL, expert_ref[...] * SL + slot, -1).astype(F32)
-    flip[1, :, 0:TOP] = gate_ref[...]
-    meta_ref[0:8] = flip[0].T[0:8]
-    meta_ref[8:16] = flip[1].T[0:8]
+    meta_ref[...] = jnp.zeros(meta_ref.shape, F32)
+    for j in range(TOP):
+        slot = slot_ref[j]
+        meta_ref[j : j + 1] = jnp.where(slot < SL, expert_ref[j] * SL + slot, -1).astype(F32)
+        meta_ref[8 + j : 9 + j] = gate_ref[j]
     for p in range(2):
         mall[p, 0] = meta_ref[...]
         for d in range(1, S):
@@ -479,7 +478,6 @@
             scratch_shapes=[
                 pltpu.VMEM((T, D), BF16),
                 pltpu.VMEM((16, T), F32),
-                pltpu.VMEM((2, T, 128), F32),
                 pltpu.VMEM((2, S - 1, T, H), BF16),
                 pltpu.VMEM((2, S, 16, T), F32),
                 pltpu.VMEM((2, rows, T), BF16),
@@ -505,7 +503,7 @@
             compiler_params=pltpu.CompilerParams(
                 collective_id=0, has_side_effects=True, vmem_limit_bytes=67043328
             ),
-        )(x.reshape(T, D), *(v.reshape(T, TOP) for v in (expert, slot, gate)), w_gate, w_up, w_down, s_gate, s_up, s_down)
+        )(x.reshape(T, D), *(v.transpose(0, 3, 1, 2).reshape(TOP, 1, T) for v in (expert, slot, gate)), w_gate, w_up, w_down, s_gate, s_up, s_down)
         return y.reshape(x.shape)
 
     own, experts, whole = P("dp", "ep"), P("ep"), P()

time: 170 us -> 165 us (0.971)
  local copies, waits for them, and re-layouts: 6.9 us -> 2.46 us
    unnamed x4 -> x1, local copies, waits for them, and re-layouts: 6.9 us -> 2.46 us
where the time goes in v3:
time: 165 us; the launch traced here: 164 us
  Pallas kernels  161 us (98%)
  local copies, waits for them, and re-layouts  2.46 us (1%)
    pallas_call x1, Pallas kernels, local(): pl.pallas_call(functools.partial(kernel, S, EPD, TOP), out_shape=jax.Shap...  161 us

profile of v3, /device:TPU:96, one launch (start us, length us, event | category | flops | bytes accessed | tf_op | source)
XLA Modules:
  0.0 163.7 jit_solution(15054303166135179279)
XLA Ops:
  0.0 161.2 %shard_map.100 = bf16[256,2560]{1,0:T(8,128)(2,1)} custom-call(bf16[256,2560]{1,0:T(8,128)(2,1)} %bitcast.12, s32[6,1,256]{2,1,0:T(1,128)} %bitcast.13, s32[6,1,256]{2,1,0:T(1,128)} %bitcast.14, f32[6,1,256]{2,1,0:T(1,128)} %bitcast.15, bf16[5,2560,1536]{2,1,0:T(8,128)(2,1)} %wg.1, bf16[5,2560,1536]{2,1,0:T(8,128)(2,1)} %wu.1, bf16[5,1536,2560]{2,1,0:T(8,128)(2,1)} %wd.1, ...), custom_call_target="tpu_custom_call" | custom-call | tf_op jit(solution)/shard_map/pallas_call | solution.py:471
  161.2 2.5 %copy.12 = bf16[1,1,256,2560]{3,2,1,0:T(8,128)(2,1)} copy(bf16[1,1,256,2560]{3,2,1,0:T(8,128)(2,1)} %bitcast.11) | data formatting | bytes 2621440

commit v4 on v3

--- a/solution.py
+++ b/solution.py
@@ -12,6 +12,7 @@
 LO, HI = 16, 8
 CT = 256
 DB = 4
+GB = 3
 EARLY = 1
 
 
@@ -25,9 +26,9 @@
 
 def kernel(
     S, EPD, TOP,
-    x_hbm, expert_ref, slot_ref, gate_ref, wg, wu, wd, sg, su, sd, y_ref,
-    x_ref, meta_ref, ag, mall, oh, dsend, z, zf, crecv, via, fin, cmat, h, ysh, gu, db,
-    x_sem, gu_sem, db_sem, ag_s, ag_r, m_s, m_r, z_s, z_r, c_s, c_r, v_s, v_r, f_s, f_r,
+    x_hbm, expert_hbm, slot_hbm, gate_hbm, wg, wu, wd, sg, su, sd, sum_ref, late_ref,
+    x_ref, expert_ref, slot_ref, gate_ref, meta_ref, ag, mall, oh, dsend, z, zf, crecv, via, fin, cmat, h, ysh, gu, db,
+    x_sem, i_sem, y_sem, gu_sem, db_sem, ag_s, ag_r, m_s, m_r, z_s, z_r, c_s, c_r, v_s, v_r, f_s, f_r,
 ):
     T, D = x_ref.shape
     FF = wg.shape[2]
@@ -54,7 +55,7 @@
         return (r // 2) * PR + 2 * LO + (r % 2) * HI
 
     def start_gu(n):
-        slot = lax.rem(n, 2)
+        slot = lax.rem(n, GB)
         u, c = lax.div(n, NG), lax.rem(n, NG)
 
         @pl.when(jnp.logical_or(u == 0, u == LAST))
@@ -69,7 +70,7 @@
             pltpu.make_async_copy(wu.at[u - 1, :, cols(c)], gu.at[slot, 1], gu_sem.at[slot, 1]).start()
 
     def wait_gu(n):
-        slot = lax.rem(n, 2)
+        slot = lax.rem(n, GB)
         for j in range(2):
             pltpu.make_async_copy(sg.at[:, cols(0)], gu.at[slot, j], gu_sem.at[slot, j]).wait()
         return slot
@@ -93,15 +94,23 @@
         return slot
 
     x_copy = pltpu.make_async_copy(x_hbm, x_ref, x_sem)
+    routing = [
+        pltpu.make_async_copy(a, b, i_sem.at[i])
+        for i, (a, b) in enumerate(
+            ((expert_hbm, expert_ref), (slot_hbm, slot_ref), (gate_hbm, gate_ref))
+        )
+    ]
+    barrier = pltpu.get_barrier_semaphore()
+    for p in range(2):
+        for d in range(1, S):
+            pl.semaphore_signal(barrier, inc=1, device_id={"ep": dev(p, d, 0)})
+    for copy in routing:
+        copy.start()
     x_copy.start()
-    start_gu(jnp.int32(0))
+    for n in range(GB - 1):
+        start_gu(jnp.int32(n))
     for m in range(DB - 1):
         start_db(jnp.int32(m))
-
-    barrier = pltpu.get_barrier_semaphore()
-    for p in range(2):
-        for d in range(1, S):
-            pl.semaphore_signal(barrier, inc=1, device_id={"ep": dev(p, d, 0)})
     pl.semaphore_wait(barrier, 2 * (S - 1))
 
     def remote(src, dst, s, r, to):
@@ -130,6 +139,8 @@
             for d in (1, S - 1):
                 ag_first(p, d, early).start()
 
+    for copy in routing:
+        copy.wait()
     meta_ref[...] = jnp.zeros(meta_ref.shape, F32)
     for j in range(TOP):
         slot = slot_ref[j]
@@ -144,7 +155,7 @@
         def tile(i, _):
             n = u * NG + i
             slot = wait_gu(n)
-            pl.when(n + 1 < (LAST + 1) * NG)(lambda: start_gu(n + 1))
+            pl.when(n + GB - 1 < (LAST + 1) * NG)(lambda: start_gu(n + GB - 1))
             g = dot(lhs[...], gu[slot, 0])
             v = dot(lhs[...], gu[slot, 1])
             h[0:rows, cols(i)] = (jax.nn.silu(g) * v).astype(BF16)
@@ -367,7 +378,10 @@
 
     def fin_copy(p, i, half):
         src = dsend.at[p, 2 * i, pl.ds(half * HT, HT)]
-        dst = fin.at[p, i, pl.ds(half * HT, HT)]
+        if half == i:
+            dst = late_ref.at[pl.ds(half * HT, HT), pl.ds(p * H, H)]
+        else:
+            dst = fin.at[p, i]
         return remote(src, dst, f_s.at[p, i, half], f_r.at[p, i, half], dev(p, 1 if i == 0 else S - 1, 0))
 
     for p in range(2):
@@ -426,18 +440,26 @@
 
         lax.fori_loop(0, HTILES, own, 0)
 
+    def y_copy(p):
+        half = pl.ds(p * H, H)
+        return pltpu.make_async_copy(ysh.at[:, half], sum_ref.at[:, half], y_sem.at[p])
+
     for p in range(2):
         for i in range(2):
-            for half in range(2):
-                fin_copy(p, i, half).wait_recv()
+            fin_copy(p, i, 1 - i).wait_recv()
 
         def last(c, _):
-            a = fin[p, 0, :, cols(c)].astype(F32) + fin[p, 1, :, cols(c)].astype(F32)
             at = cols(p * HTILES + c)
-            y_ref[:, at] = (ysh[:, at] + a).astype(y_ref.dtype)
+            ysh[0:HT, at] += fin[p, 1, :, cols(c)].astype(F32)
+            ysh[HT:T, at] += fin[p, 0, :, cols(c)].astype(F32)
             return 0
 
         lax.fori_loop(0, HTILES, last, 0)
+        y_copy(p).start()
+    for p in range(2):
+        y_copy(p).wait()
+        for i in range(2):
+            fin_copy(p, i, i).wait_recv()
 
     for p in range(2):
         for d in range(1, S):
@@ -468,15 +490,16 @@
         assert FF * 2 == s_gate.shape[1] and SL == 5 * T * TOP // (4 * EPD * mesh.shape["ep"])
         rows = EPD * S * SL
         sem = pltpu.SemaphoreType.DMA
-        y = pl.pallas_call(
+        total, late = pl.pallas_call(
             functools.partial(kernel, S, EPD, TOP),
-            out_shape=jax.ShapeDtypeStruct((T, D), x.dtype),
-            in_specs=[pl.BlockSpec(memory_space=pl.ANY)]
-            + [pl.BlockSpec(memory_space=pltpu.VMEM)] * 3
-            + [pl.BlockSpec(memory_space=pl.ANY)] * 6,
-            out_specs=pl.BlockSpec(memory_space=pltpu.VMEM),
+            out_shape=[jax.ShapeDtypeStruct((T, D), F32), jax.ShapeDtypeStruct((T, D), BF16)],
+            in_specs=[pl.BlockSpec(memory_space=pl.ANY)] * 10,
+            out_specs=[pl.BlockSpec(memory_space=pl.ANY)] * 2,
             scratch_shapes=[
                 pltpu.VMEM((T, D), BF16),
+                pltpu.VMEM((TOP, 1, T), jnp.int32),
+                pltpu.VMEM((TOP, 1, T), jnp.int32),
+                pltpu.VMEM((TOP, 1, T), F32),
                 pltpu.VMEM((16, T), F32),
                 pltpu.VMEM((2, S - 1, T, H), BF16),
                 pltpu.VMEM((2, S, 16, T), F32),
@@ -486,13 +509,13 @@
                 pltpu.VMEM((S * S * SL, D), BF16),
                 pltpu.VMEM((2, EPD, S, S * SL, H), BF16),
                 pltpu.VMEM((2, 2, T // 2, H), BF16),
-                pltpu.VMEM((2, 2, T, H), BF16),
+                pltpu.VMEM((2, 2, T // 2, H), BF16),
                 pltpu.VMEM((2, S, T, 2 * EPD * S * LO), BF16),
                 pltpu.VMEM((S * S * SL, FF), BF16),
                 pltpu.VMEM((T, D), F32),
-                pltpu.VMEM((2, 2, D, CT), BF16),
+                pltpu.VMEM((GB, 2, D, CT), BF16),
                 pltpu.VMEM((DB, FF, CT), BF16),
-                sem, sem((2, 2)), sem((DB,)),
+                sem, sem((3,)), sem((2,)), sem((GB, 2)), sem((DB,)),
                 sem((2, 6)), sem((2, 6)),
                 sem((2, S - 1)), sem((2, S - 1)),
                 sem((2, EPD, S - 1, 2)), sem((2, EPD, S - 1, 2)),
@@ -504,7 +527,7 @@
                 collective_id=0, has_side_effects=True, vmem_limit_bytes=67043328
             ),
         )(x.reshape(T, D), *(v.transpose(0, 3, 1, 2).reshape(TOP, 1, T) for v in (expert, slot, gate)), w_gate, w_up, w_down, s_gate, s_up, s_down)
-        return y.reshape(x.shape)
+        return (total + late.astype(F32)).astype(x.dtype).reshape(x.shape)
 
     own, experts, whole = P("dp", "ep"), P("ep"), P()
     return jax.shard_map(

time: 165 us -> 163 us (0.988)
  other arithmetic: 0 us -> 3.46 us
  local copies, waits for them, and re-layouts: 2.46 us -> 0 us
  Pallas kernels: 161 us -> 159 us
    reshape x0 -> x1, other arithmetic: none -> 3.46 us  [local(): return (total + late.astype(F32)).astype(x.dtype).reshape(x.shape)]
    unnamed x1 -> x0, local copies, waits for them, and re-layouts: 2.46 us -> none
    pallas_call x1, Pallas kernels: 161 us -> 159 us  [local(): pl.pallas_call(functools.partial(kernel, S, EPD, TOP), out_shape=[jax.Sha...]
where the time goes in v4:
time: 163 us; the launch traced here: 162 us
  Pallas kernels  159 us (98%)
  other arithmetic  3.46 us (2%)
    pallas_call x1, Pallas kernels, local(): pl.pallas_call(functools.partial(kernel, S, EPD, TOP), out_shape=[jax.Sha...  159 us
    reshape x1, other arithmetic, local(): return (total + late.astype(F32)).astype(x.dtype).reshape(x.shape)  3.46 us

profile of v4, /device:TPU:96, one launch (start us, length us, event | category | flops | bytes accessed | tf_op | source)
XLA Modules:
  0.0 162.4 jit_solution(755658787941606184)
XLA Ops:
  0.0 159.0 %shard_map.100 = (f32[256,2560]{1,0:T(8,128)}, bf16[256,2560]{1,0:T(8,128)(2,1)}) custom-call(bf16[256,2560]{1,0:T(8,128)(2,1)} %bitcast.12, s32[6,1,256]{2,1,0:T(1,128)} %bitcast.13, s32[6,1,256]{2,1,0:T(1,128)} %bitcast.14, f32[6,1,256]{2,1,0:T(1,128)} %bitcast.15, bf16[5,2560,1536]{2,1,0:T(8,128)(2,1)} %wg.1, bf16[5,2560,1536]{2,1,0:T(8,128)(2,1)} %wu.1, ...), custom_call_target="tpu_custom_call" | custom-call | tf_op jit(solution)/shard_map/pallas_call | solution.py:493
  159.0 3.5 %fusion = bf16[1,1,256,2560]{3,2,1,0:T(8,128)(2,1)} fusion(f32[256,2560]{1,0:T(8,128)} %get-tuple-element.7, bf16[256,2560]{1,0:T(8,128)(2,1)} %get-tuple-element.8), kind=kLoop, calls=%fused_computation.1 | loop fusion | flops 1966080 | bytes 5242880 | tf_op jit(solution)/shard_map/reshape | solution.py:530

commit v5 on v4

--- a/solution.py
+++ b/solution.py
@@ -11,6 +11,7 @@
 F32, BF16 = jnp.float32, jnp.bfloat16
 LO, HI = 16, 8
 CT = 256
+PARTS = 2
 DB = 4
 GB = 3
 EARLY = 1
@@ -476,6 +477,10 @@
             via_copy(p, i).wait_send()
             for half in range(2):
                 fin_copy(p, i, half).wait_send()
+
+
+def add(a_ref, b_ref, y_ref):
+    y_ref[...] = (a_ref[...] + b_ref[...].astype(F32)).astype(y_ref.dtype)
 
 
 def solution(mesh):
@@ -527,7 +532,14 @@
                 collective_id=0, has_side_effects=True, vmem_limit_bytes=67043328
             ),
         )(x.reshape(T, D), *(v.transpose(0, 3, 1, 2).reshape(TOP, 1, T) for v in (expert, slot, gate)), w_gate, w_up, w_down, s_gate, s_up, s_down)
-        return (total + late.astype(F32)).astype(x.dtype).reshape(x.shape)
+        y = pl.pallas_call(
+            add,
+            grid=(PARTS,),
+            out_shape=jax.ShapeDtypeStruct((T, D), x.dtype),
+            in_specs=[pl.BlockSpec((T // PARTS, D), lambda i: (i, 0))] * 2,
+            out_specs=pl.BlockSpec((T // PARTS, D), lambda i: (i, 0)),
+        )(total, late)
+        return y.reshape(x.shape)
 
     own, experts, whole = P("dp", "ep"), P("ep"), P()
     return jax.shard_map(

time: 163 us -> 162 us (level)
  other arithmetic: 3.46 us -> 0 us
  Pallas kernels: 159 us -> 162 us
    reshape x1 -> x0, other arithmetic: 3.46 us -> none  [local(): return (total + late.astype(F32)).astype(x.dtype).reshape(x.shape)]
    pallas_call x0 -> x1, Pallas kernels: none -> 3.03 us  [local(): pl.pallas_call(add, grid=(PARTS,), out_shape=jax.ShapeDtypeStruct((T, D),...]
where the time goes in v5:
time: 162 us
  Pallas kernels  162 us (100%)
    pallas_call x1, Pallas kernels, local(): pl.pallas_call(functools.partial(kernel, S, EPD, TOP), out_shape=[jax.Sha...  159 us

profile of v5, /device:TPU:96, one launch (start us, length us, event | category | flops | bytes accessed | tf_op | source)
XLA Modules:
  0.0 162.0 jit_solution(6850556418561297227)
XLA Ops:
  0.0 159.0 %shard_map.100 = (f32[256,2560]{1,0:T(8,128)}, bf16[256,2560]{1,0:T(8,128)(2,1)}) custom-call(bf16[256,2560]{1,0:T(8,128)(2,1)} %bitcast.11, s32[6,1,256]{2,1,0:T(1,128)} %bitcast.12, s32[6,1,256]{2,1,0:T(1,128)} %bitcast.13, f32[6,1,256]{2,1,0:T(1,128)} %bitcast.14, bf16[5,2560,1536]{2,1,0:T(8,128)(2,1)} %wg.1, bf16[5,2560,1536]{2,1,0:T(8,128)(2,1)} %wu.1, ...), custom_call_target="tpu_custom_call" | custom-call | tf_op jit(solution)/shard_map/pallas_call | solution.py:498
  159.0 3.0 %shard_map.101 = bf16[256,2560]{1,0:T(8,128)(2,1)} custom-call(f32[256,2560]{1,0:T(8,128)} %get-tuple-element.7.a_ref, bf16[256,2560]{1,0:T(8,128)(2,1)} %get-tuple-element.8.b_ref), custom_call_target="tpu_custom_call" | custom-call | tf_op jit(solution)/shard_map/pallas_call | solution.py:535
